TPU v7x, 512 devices: a whole 4x4x16 slice. The times are simulated.
512 devices in a mesh: vit: 8 (over z_hi, y), seq: 8 (over z_lo), tensor: 8 (over x, core).
Axes of the slice: x: 4, y: 4, z: 16 (z_hi: 2, z_lo: 8; z = z_hi * 8 + z_lo), core: 2. Of those that a mesh axis runs over, the one named last changes fastest.
Arguments:
- merged: bfloat16 [2048, 8192], P(('vit', 'seq'), 'tensor'), may hold values from -6 to 6
- positions: int32 [2048], P(('vit', 'seq')), may hold values from 0 to 131071, as said below
- picked: int32 [2048], P(('vit', 'seq')), may hold values from 0 to 1, as said below
- router_score: float32 [2048], P(('vit', 'seq')), may hold values from -8 to 8
- up_weight: bfloat16 [8192, 16384], P('tensor', ('vit', 'seq')), may hold values from -0.0625 to 0.0625
- down_weight: bfloat16 [16384, 8192], P(('vit', 'seq'), 'tensor'), may hold values from -0.046875 to 0.046875
- mixed_grad: bfloat16 [1024, 8192], P(('vit', 'seq'), 'tensor'), may hold values from -6 to 6
Outputs:
- mixed: bfloat16 [1024, 8192], P(('vit', 'seq'), 'tensor')
- token_grad: bfloat16 [2048, 8192], P(('vit', 'seq'), 'tensor')
- up_grad: float32 [8192, 16384], P('tensor', ('vit', 'seq'))
- down_grad: float32 [16384, 8192], P(('vit', 'seq'), 'tensor')
Inputs may be any that keep to these rules, and one draw needn't show every extreme that they name: Among the picked tokens of one aligned block of 32 tokens, at most 2 have the same positions // 16384, and in every block some value of positions // 16384 is shared by exactly 2 picked tokens. `picked`: exactly 8 ones in every aligned block of 32 tokens.
All inputs are finite; a program needn't handle non-finite values.
Results may differ from a plain program's by a relative error of at most 0.0056.
Values may be sent and summed in bfloat16 or wider, within the bound.
A program may use at most 64 MiB of HBM per device.

v0:
```python
import jax
import jax.numpy as jnp
from jax import lax
from jax.sharding import Mesh
from jax.sharding import PartitionSpec as P

CAP = 2
SPAN = 16384
VIT_SEQ = ("vit_0", "vit_1", "seq")


def laid_out(parts, dim):
    lengths = list(parts.shape[1:])
    lengths[dim] *= parts.shape[0]
    return jnp.moveaxis(parts, 0, dim).reshape(lengths)


def gather_in_order(x, axes, order):
    parts = x
    for k in order:
        parts = lax.all_gather(parts, axes[k])
    done = order[::-1]
    back = [done.index(k) for k in range(len(axes))]
    parts = parts.transpose(*back, *range(len(axes), parts.ndim))
    return parts.reshape(-1, *x.shape)


def whole_of(x, axes, order, dim):
    return laid_out(gather_in_order(x, axes, order), dim)


def split_up(x, dim, count):
    before, after = (x.shape[:dim], x.shape[dim + 1 :])
    return jnp.moveaxis(x.reshape(*before, count, -1, *after), dim, 0)


def sum_at_owner(x, axis, dim):
    parts = split_up(x, dim, lax.axis_size(axis))
    arrived = lax.all_to_all(parts, axis, split_axis=0, concat_axis=0, tiled=True)
    return arrived.sum(axis=0)


def sent_to_all(x, axis):
    count = lax.axis_size(axis)
    return lax.all_to_all(jnp.broadcast_to(x[None], (count, *x.shape)), axis, 0, 0, tiled=True)


def collect(x, axis, dim):
    parts = sent_to_all(x, axis)
    return laid_out(parts, dim)


def build_place(positions, picked, slot_count):
    seqs = lax.axis_size("seq")
    target = positions // SPAN
    owners = jnp.arange(seqs, dtype=jnp.int32)
    onehot = (target[:, None] == owners[None, :]).astype(jnp.int32) * picked[:, None]
    ranks = jnp.sum((jnp.cumsum(onehot, axis=0) - onehot) * onehot, axis=1)
    slot = target * CAP + ranks
    wanted = jnp.arange(slot_count, dtype=jnp.int32)
    return ((slot[:, None] == wanted[None, :]) & (picked[:, None] == 1)).astype(jnp.bfloat16)


def spread(local_rows):
    return whole_of(local_rows, VIT_SEQ, (0, 2, 1), 0)


def reduce_hidden(partial_value):
    summed = sum_at_owner(partial_value, "tensor", 0)
    return summed


def widen(values):
    whole = collect(values, "tensor", 0)
    return whole


def row_sum(left, right, contract, local_count):
    term = lax.dot_general(
        left, right, (((1,), (contract,)), ((), ())), preferred_element_type=jnp.float32
    ).astype(jnp.bfloat16)
    pieces = term.reshape(-1, local_count, term.shape[1])
    arrived = lax.all_to_all(pieces, VIT_SEQ, split_axis=0, concat_axis=0, tiled=True)
    return jnp.sum(arrived.astype(jnp.float32), axis=0)


def layer_pass(local_rows, local_gates, cotangent_of, up_weight, down_weight):
    local_count = local_rows.shape[0]
    every_row = spread(local_rows)
    pre = reduce_hidden(jnp.dot(every_row, up_weight, preferred_element_type=jnp.float32))
    act = widen(jax.nn.silu(pre).astype(jnp.bfloat16))
    y_rows = row_sum(act, down_weight, 0, local_count)
    gates_wide = local_gates.astype(jnp.float32)[:, None]
    out_rows = (local_rows.astype(jnp.float32) + gates_wide * y_rows).astype(jnp.bfloat16)
    cotangent = cotangent_of(out_rows)
    scaled = (gates_wide * cotangent.astype(jnp.float32)).astype(jnp.bfloat16)
    every_scaled = spread(scaled)
    down_grad = lax.dot_general(
        act, every_scaled, (((0,), (0,)), ((), ())), preferred_element_type=jnp.float32
    )
    act_grad = reduce_hidden(
        lax.dot_general(
            every_scaled, down_weight, (((1,), (1,)), ((), ())), preferred_element_type=jnp.float32
        )
    )
    sig = jax.nn.sigmoid(pre)
    pre_grad = widen((act_grad * sig * (1.0 + pre * (1.0 - sig))).astype(jnp.bfloat16))
    up_grad = lax.dot_general(
        every_row, pre_grad, (((0,), (0,)), ((), ())), preferred_element_type=jnp.float32
    )
    row_grad = row_sum(pre_grad, up_weight, 1, local_count)
    slot_grad = (cotangent.astype(jnp.float32) + row_grad).astype(jnp.bfloat16)
    return (out_rows, slot_grad, up_grad, down_grad)


def per_device(merged, positions, picked, router_score, up_weight, down_weight, mixed_grad):
    slot_count = mixed_grad.shape[0]
    place = build_place(positions, picked, slot_count)
    send_rows = jnp.dot(place.T, merged, preferred_element_type=jnp.float32).astype(jnp.bfloat16)
    gate_tok = jax.nn.sigmoid(router_score).astype(jnp.bfloat16)
    send_gates = jnp.dot(place.T, gate_tok[:, None], preferred_element_type=jnp.float32)[
        :, 0
    ].astype(jnp.bfloat16)
    cotangent_here = lax.all_to_all(mixed_grad, "seq", split_axis=0, concat_axis=0, tiled=True)

    def fetched(out_rows):
        return cotangent_here

    out_rows, returned, up_grad, down_grad = layer_pass(
        send_rows, send_gates, fetched, up_weight, down_weight
    )
    mixed = lax.all_to_all(out_rows, "seq", split_axis=0, concat_axis=0, tiled=True)
    token_grad = jnp.dot(place, returned, preferred_element_type=jnp.float32).astype(jnp.bfloat16)
    return (mixed, token_grad, up_grad, down_grad)


def solution(mesh):
    finer = Mesh(
        mesh.devices.reshape(2, 4, mesh.shape["seq"], mesh.shape["tensor"]),
        ("vit_0", "vit_1", "seq", "tensor"),
    )
    placed = (
        P(VIT_SEQ, "tensor"),
        P(VIT_SEQ),
        P(VIT_SEQ),
        P(VIT_SEQ),
        P("tensor", VIT_SEQ),
        P(VIT_SEQ, "tensor"),
        P(VIT_SEQ, "tensor"),
    )
    return jax.shard_map(
        per_device,
        mesh=finer,
        in_specs=placed,
        out_specs=(
            P(VIT_SEQ, "tensor"),
            P(VIT_SEQ, "tensor"),
            P("tensor", VIT_SEQ),
            P(VIT_SEQ, "tensor"),
        ),
        check_vma=False,
    )
```

profile of v0, /device:TPU:1, one launch (start us, length us, event | category | flops | bytes accessed | tf_op | source)
XLA Modules:
  0.0 491.8 jit_solution(1674793750606403615)
XLA Ops:
  12.0 16.4 %all-gather = bf16[32,1024]{1,0:T(8,128)(2,1)S(1)} all-gather(bf16[16,1024]{1,0:T(8,128)(2,1)S(1)} %convolution_convert_fusion.3), channel_id=2, replica_groups=mesh['vit_0'=2,'vit_1'=4,'seq'=8,'tensor'=8] {'vit_0'}, dimensions={0}, use_global_device_ids=true | all-gather | bytes 98304 | tf_op jit(solution)/shard_map/all_gather | solution.py:21
  28.4 45.9 %all-gather.1 = bf16[16,16,1024]{2,1,0:T(8,128)(2,1)} all-gather(bf16[2,16,1024]{2,1,0:T(8,128)(2,1)S(1)} %bitcast.57), channel_id=3, replica_groups=mesh['vit_0'=2,'vit_1'=4,'seq'=8,'tensor'=8] {'seq'}, dimensions={0}, use_global_device_ids=true | all-gather | bytes 589824 | tf_op jit(solution)/shard_map/all_gather | solution.py:21
  75.7 6.7 %all-to-all-start.4 = ((bf16[8,2,1024]{2,1,0:T(2,128)(2,1)}), bf16[8,2,1024]{2,1,0:T(2,128)(2,1)S(1)}, u32[]{:S(2)}, u32[]{:S(2)}) async-start(bf16[8,2,1024]{2,1,0:T(2,128)(2,1)} %all_to_all.38), calls=%async_computation.4 | async-start | bytes 65536 | tf_op jit(solution)/shard_map/all_to_all | solution.py:124
  83.2 8.6 %all-to-all-done.4 = bf16[8,2,1024]{2,1,0:T(2,128)(2,1)S(1)} async-done(((bf16[8,2,1024]{2,1,0:T(2,128)(2,1)}), bf16[8,2,1024]{2,1,0:T(2,128)(2,1)S(1)}, u32[]{:S(2)}, u32[]{:S(2)}) %all-to-all-start.4) | async-done | bytes 32800 | tf_op jit(solution)/shard_map/all_to_all | solution.py:124
  91.9 12.1 %all_gather.40 = bf16[2,16,1024]{2,1,0:T(8,128)(2,1)S(1)} all-gather(bf16[1,16,1024]{2,1,0:T(8,128)(2,1)S(1)} %multiply_convert_fusion.2), channel_id=1, replica_groups=mesh['vit_0'=2,'vit_1'=4,'seq'=8,'tensor'=8] {'vit_0'}, dimensions={0}, use_global_device_ids=true | all-gather | bytes 98304 | tf_op jit(solution)/shard_map/all_gather | solution.py:21
  104.1 44.6 %all-gather.3 = bf16[16,16,1024]{2,1,0:T(8,128)(2,1)} all-gather(bf16[2,16,1024]{2,1,0:T(8,128)(2,1)S(1)} %all_gather.40), channel_id=5, replica_groups=mesh['vit_0'=2,'vit_1'=4,'seq'=8,'tensor'=8] {'seq'}, dimensions={0}, use_global_device_ids=true | all-gather | bytes 589824 | tf_op jit(solution)/shard_map/all_gather | solution.py:21
  153.6 21.3 %all-to-all-start = ((f32[8,128,256]{2,1,0:T(8,128)}), f32[8,128,256]{2,1,0:T(8,128)}, u32[]{:S(2)}, u32[]{:S(2)}) async-start(f32[8,128,256]{2,1,0:T(8,128)} %fusion.4), calls=%async_computation | async-start | bytes 2097152 | tf_op jit(solution)/shard_map/all_to_all | solution.py:39
  174.9 25.7 %all-gather.10.cloned.1.call-done = bf16[32,2,16,1024]{3,2,1,0:T(8,128)(2,1)} async-done(((bf16[8,2,16,1024]{3,2,1,0:T(8,128)(2,1)}), bf16[32,2,16,1024]{3,2,1,0:T(8,128)(2,1)}) %all-gather.10.cloned.1.call-update) | async-done | bytes 2097168 | tf_op jit(solution)/shard_map/all_gather | solution.py:21
  204.1 5.1 %all-to-all-start.5 = ((f32[8,128,256]{2,1,0:T(8,128)}), f32[8,128,256]{2,1,0:T(8,128)}, u32[]{:S(2)}, u32[]{:S(2)}) async-start(f32[8,128,256]{2,1,0:T(8,128)} %fusion.2), calls=%async_computation.5 | async-start | bytes 2097152 | tf_op jit(solution)/shard_map/all_to_all | solution.py:39
  210.5 13.8 %all-to-all-done.5 = f32[8,128,256]{2,1,0:T(8,128)} async-done(((f32[8,128,256]{2,1,0:T(8,128)}), f32[8,128,256]{2,1,0:T(8,128)}, u32[]{:S(2)}, u32[]{:S(2)}) %all-to-all-start.5) | async-done | bytes 1048608 | tf_op jit(solution)/shard_map/all_to_all | solution.py:39
  225.7 12.7 %all_to_all.51 = bf16[8,128,256]{2,1,0:T(8,128)(2,1)S(1)} all-to-all(bf16[8,128,256]{2,1,0:T(8,128)(2,1)S(1)} %broadcast_in_dim.4), channel_id=1, replica_groups=mesh['vit_0'=2,'vit_1'=4,'seq'=8,'tensor'=8] {'tensor'}, dimensions={0} | all-to-all | bytes 1048576 | tf_op jit(solution)/shard_map/all_to_all | solution.py:45
  239.2 5.1 %all-to-all-start.6 = ((bf16[8,128,256]{2,1,0:T(8,128)(2,1)}), bf16[8,128,256]{2,1,0:T(8,128)(2,1)}, u32[]{:S(2)}, u32[]{:S(2)}) async-start(bf16[8,128,256]{2,1,0:T(8,128)(2,1)} %broadcast_in_dim.5), calls=%async_computation.6 | async-start | bytes 1048576 | tf_op jit(solution)/shard_map/all_to_all | solution.py:45
  244.3 2.1 convolution_convert_fusion.1
  246.3 7.4 %all-to-all-done.6 = bf16[8,128,256]{2,1,0:T(8,128)(2,1)} async-done(((bf16[8,128,256]{2,1,0:T(8,128)(2,1)}), bf16[8,128,256]{2,1,0:T(8,128)(2,1)}, u32[]{:S(2)}, u32[]{:S(2)}) %all-to-all-start.6) | async-done | bytes 524320 | tf_op jit(solution)/shard_map/all_to_all | solution.py:45
  253.8 14.4 %all-to-all-start.2 = ((bf16[64,16,1024]{2,1,0:T(8,128)(2,1)}), bf16[64,16,1024]{2,1,0:T(8,128)(2,1)}, u32[]{:S(2)}, u32[]{:S(2)}) async-start(bf16[64,16,1024]{2,1,0:T(8,128)(2,1)} %bitcast.50), calls=%async_computation.2 | async-start | bytes 4194304 | tf_op jit(solution)/shard_map/all_to_all | solution.py:83
  268.1 3.3 convolution_convert_fusion
  271.4 92.0 %all-to-all-done.2 = bf16[64,16,1024]{2,1,0:T(8,128)(2,1)} async-done(((bf16[64,16,1024]{2,1,0:T(8,128)(2,1)}), bf16[64,16,1024]{2,1,0:T(8,128)(2,1)}, u32[]{:S(2)}, u32[]{:S(2)}) %all-to-all-start.2) | async-done | bytes 2097184 | tf_op jit(solution)/shard_map/all_to_all | solution.py:83
  363.4 10.4 %all-to-all-start.7 = ((bf16[64,16,1024]{2,1,0:T(8,128)(2,1)}), bf16[64,16,1024]{2,1,0:T(8,128)(2,1)}, u32[]{:S(2)}, u32[]{:S(2)}) async-start(bf16[64,16,1024]{2,1,0:T(8,128)(2,1)} %bitcast.49), calls=%async_computation.7 | async-start | bytes 4194304 | tf_op jit(solution)/shard_map/all_to_all | solution.py:83
  373.8 3.4 fusion.24
  378.9 2.0 convert_reduce_fusion.1
  381.6 87.6 %all-to-all-done.7 = bf16[64,16,1024]{2,1,0:T(8,128)(2,1)} async-done(((bf16[64,16,1024]{2,1,0:T(8,128)(2,1)}), bf16[64,16,1024]{2,1,0:T(8,128)(2,1)}, u32[]{:S(2)}, u32[]{:S(2)}) %all-to-all-start.7) | async-done | bytes 2097184 | tf_op jit(solution)/shard_map/all_to_all | solution.py:83
  469.2 5.7 %all-to-all-start.3 = ((bf16[8,2,1024]{2,1,0:T(2,128)(2,1)}), bf16[8,2,1024]{2,1,0:T(2,128)(2,1)S(1)}, u32[]{:S(2)}, u32[]{:S(2)}) async-start(bf16[8,2,1024]{2,1,0:T(2,128)(2,1)} %all_to_all.35), calls=%async_computation.3 | async-start | bytes 65536 | tf_op jit(solution)/shard_map/all_to_all | solution.py:132
  474.8 2.0 convert_reduce_fusion
  477.6 6.7 %all-to-all-done.3 = bf16[8,2,1024]{2,1,0:T(2,128)(2,1)S(1)} async-done(((bf16[8,2,1024]{2,1,0:T(2,128)(2,1)}), bf16[8,2,1024]{2,1,0:T(2,128)(2,1)S(1)}, u32[]{:S(2)}, u32[]{:S(2)}) %all-to-all-start.3) | async-done | bytes 32800 | tf_op jit(solution)/shard_map/all_to_all | solution.py:132
  (38 shorter events, 23.0 us)
Async XLA Ops:
  7.2 195.2 %copy-start = (bf16[256,1024]{1,0:T(8,128)(2,1)S(1)}, bf16[256,1024]{1,0:T(8,128)(2,1)}, u32[]{:S(2)}) copy-start(bf16[256,1024]{1,0:T(8,128)(2,1)} %param.12) | copy-start | bytes 1572868
  7.2 141.5 %all-gather.8.cloned.1.call-start = ((), (), s32[]{:S(2)}) async-start(), calls=%async_computation.8 | async-start | bytes 2621440 | tf_op jit(solution)/shard_map/all_gather | solution.py:21
  75.7 16.1 %all-to-all-start.4 = ((bf16[8,2,1024]{2,1,0:T(2,128)(2,1)}), bf16[8,2,1024]{2,1,0:T(2,128)(2,1)S(1)}, u32[]{:S(2)}, u32[]{:S(2)}) async-start(bf16[8,2,1024]{2,1,0:T(2,128)(2,1)} %all_to_all.38), calls=%async_computation.4 | async-start | bytes 65536 | tf_op jit(solution)/shard_map/all_to_all | solution.py:124
  82.4 118.2 %all-gather.10.cloned.1.call-start = ((), (), s32[]{:S(2)}) async-start(), calls=%async_computation.9 | async-start | bytes 2621440 | tf_op jit(solution)/shard_map/all_gather | solution.py:21
  148.7 3.2 copy-start.2
  150.5 1.4 copy-start.1
  153.6 50.5 %all-to-all-start = ((f32[8,128,256]{2,1,0:T(8,128)}), f32[8,128,256]{2,1,0:T(8,128)}, u32[]{:S(2)}, u32[]{:S(2)}) async-start(f32[8,128,256]{2,1,0:T(8,128)} %fusion.4), calls=%async_computation | async-start | bytes 2097152 | tf_op jit(solution)/shard_map/all_to_all | solution.py:39
  204.1 20.2 %all-to-all-start.5 = ((f32[8,128,256]{2,1,0:T(8,128)}), f32[8,128,256]{2,1,0:T(8,128)}, u32[]{:S(2)}, u32[]{:S(2)}) async-start(f32[8,128,256]{2,1,0:T(8,128)} %fusion.2), calls=%async_computation.5 | async-start | bytes 2097152 | tf_op jit(solution)/shard_map/all_to_all | solution.py:39
  239.2 14.6 %all-to-all-start.6 = ((bf16[8,128,256]{2,1,0:T(8,128)(2,1)}), bf16[8,128,256]{2,1,0:T(8,128)(2,1)}, u32[]{:S(2)}, u32[]{:S(2)}) async-start(bf16[8,128,256]{2,1,0:T(8,128)(2,1)} %broadcast_in_dim.5), calls=%async_computation.6 | async-start | bytes 1048576 | tf_op jit(solution)/shard_map/all_to_all | solution.py:45
  253.8 109.7 %all-to-all-start.2 = ((bf16[64,16,1024]{2,1,0:T(8,128)(2,1)}), bf16[64,16,1024]{2,1,0:T(8,128)(2,1)}, u32[]{:S(2)}, u32[]{:S(2)}) async-start(bf16[64,16,1024]{2,1,0:T(8,128)(2,1)} %bitcast.50), calls=%async_computation.2 | async-start | bytes 4194304 | tf_op jit(solution)/shard_map/all_to_all | solution.py:83
  363.4 105.8 %all-to-all-start.7 = ((bf16[64,16,1024]{2,1,0:T(8,128)(2,1)}), bf16[64,16,1024]{2,1,0:T(8,128)(2,1)}, u32[]{:S(2)}, u32[]{:S(2)}) async-start(bf16[64,16,1024]{2,1,0:T(8,128)(2,1)} %bitcast.49), calls=%async_computation.7 | async-start | bytes 4194304 | tf_op jit(solution)/shard_map/all_to_all | solution.py:83
  469.2 15.1 %all-to-all-start.3 = ((bf16[8,2,1024]{2,1,0:T(2,128)(2,1)}), bf16[8,2,1024]{2,1,0:T(2,128)(2,1)S(1)}, u32[]{:S(2)}, u32[]{:S(2)}) async-start(bf16[8,2,1024]{2,1,0:T(2,128)(2,1)} %all_to_all.35), calls=%async_computation.3 | async-start | bytes 65536 | tf_op jit(solution)/shard_map/all_to_all | solution.py:132
Sparse Core Ops, SparseCore 0:
  74.4 44.7 all-gather.7
  148.8 51.7 all-gather.9
where the time goes:
time: 496 us; the launch traced here: 492 us
  waiting for transfers between devices  242 us (49%)
  blocking collectives  132 us (27%)
  starting transfers between devices  68.6 us (14%)
  matrix products  16.6 us (3%)
  between operations  14.2 us (3%)
  other arithmetic  10.4 us (2%)
  local copies, waits for them, and re-layouts  8.5 us (2%)
    all_to_all x2, waiting for transfers between devices, row_sum(): lax.all_to_all(pieces, VIT_SEQ, split_axis=0, concat_axis=0, tiled=True)  180 us
    all_gather x4, blocking collectives, gather_in_order(): parts = lax.all_gather(parts, axes[k])  119 us
    all_to_all x2, starting transfers between devices, sum_at_owner(): lax.all_to_all(parts, axis, split_axis=0, concat_axis=0, tiled=True)  26.4 us
    all_gather x2, waiting for transfers between devices, gather_in_order(): parts = lax.all_gather(parts, axes[k])  25.7 us
    all_to_all x2, starting transfers between devices, row_sum(): lax.all_to_all(pieces, VIT_SEQ, split_axis=0, concat_axis=0, tiled=True)  24.8 us
    all_to_all x2, waiting for transfers between devices, sum_at_owner(): lax.all_to_all(parts, axis, split_axis=0, concat_axis=0, tiled=True)  13.8 us
    all_to_all x1, blocking collectives, sent_to_all(): lax.all_to_all(jnp.broadcast_to(x[None], (count, *x.shape)), axis, 0, 0,...  12.7 us
  transfers between devices with their start and end apart: 9, of which 7 were waited for; matrix products, arithmetic and copies ran while one was open for 5% of the time, Pallas kernels for 0%

commit v1 on v0

v1 whole, which is shorter than its diff:
```python
import functools

import jax
import jax.numpy as jnp
from jax import lax
from jax.experimental import pallas as pl
from jax.experimental.pallas import tpu as pltpu
from jax.sharding import PartitionSpec as P

MESH = pl.DeviceIdType.MESH
F32 = jnp.float32
BF16 = jnp.bfloat16
VIT_SEQ = ("vit", "seq")

GROUPS = ((0, 1), (1, 5), (5, 8), (12, 16), (8, 12))
OWN, NEAR_P, FAR_P, NEAR_M, FAR_M = range(5)


def mm(a, b, ca=1, cb=0):
    return lax.dot_general(a, b, (((ca,), (cb,)), ((), ())), preferred_element_type=F32)


def kernel(
    merged, pos, picked, score, cot_in, up_hbm, down_hbm,
    mixed_out, token_out, up_out, down_out,
    up_w, down_w, rows_g, scaled_g, part, part_in, share, share_in, act_g, pg_g,
    terms, y_in, rb, rf, far_p, far_m, fin, relay,
    cot_send, cot_recv, mix_send, mix_recv, up_acc, down_acc,
    local_sem, ag_zrecv, ag_yrecv, ag_send, rs_yrecv, rs_zrecv, rs_send, x_sem, a_sem,
):
    vit, seq, ten = (lax.axis_index(a) for a in ("vit", "seq", "tensor"))
    z = (vit // 4) * 8 + seq
    y = vit % 4
    x, core = ten // 2, ten % 2

    def at_z(k):
        other = (z + k + 16) % 16
        return ((other // 8) * 4 + y, other % 8, ten)

    def at_y(k):
        return ((vit // 4) * 4 + (y + k + 4) % 4, seq, ten)

    def at_ten(k):
        return (vit, seq, (ten + k) % 8)

    def at_x(k):
        return (vit, seq, ((x + k) % 4) * 2 + core)

    partner = (vit, seq, x * 2 + 1 - core)

    def at_seq(k):
        return (vit, (seq + k) % 8, ten)

    def remote(src, dst, send, recv, to):
        return pltpu.make_async_remote_copy(
            src_ref=src, dst_ref=dst, send_sem=send, recv_sem=recv, device_id=to, device_id_type=MESH
        )

    def push(src, dst, send, recv, to):
        remote(src, dst, send, recv, to).start()

    def got(dst, recv):
        remote(dst, dst, recv, recv, partner).wait_recv()

    def sent(src, send):
        remote(src, src, send, send, partner).wait_send()

    load_up = pltpu.make_async_copy(up_hbm, up_w, local_sem.at[0])
    load_down = pltpu.make_async_copy(down_hbm, down_w, local_sem.at[1])
    load_up.start()
    load_down.start()

    barrier = pltpu.get_barrier_semaphore()
    peers = [at_z(k) for k in (4, -4, 3, -3, 2, -2, 1, -1)]
    peers += [at_y(1), at_y(-1)]
    peers += [at_ten(k) for k in range(1, 8)]
    peers += [at_seq(k) for k in range(1, 8)]
    for peer in peers:
        pl.semaphore_signal(barrier, inc=1, device_id=peer, device_id_type=MESH)

    n = pos.shape[1]
    t_row = (pos[...] >> 14).astype(F32)
    p_row = picked[...].astype(F32)
    i0 = lax.broadcasted_iota(jnp.int32, (n, n), 0)
    i1 = lax.broadcasted_iota(jnp.int32, (n, n), 1)
    eye = i0 == i1
    t_wide = jnp.broadcast_to(t_row, (n, n))
    p_wide = jnp.broadcast_to(p_row, (n, n))
    t_col = jnp.sum(jnp.where(eye, t_wide, 0.0), axis=1, keepdims=True)
    p_col = jnp.sum(jnp.where(eye, p_wide, 0.0), axis=1, keepdims=True)
    same = t_col == t_wide
    c_row = jnp.sum(jnp.where(i0 < i1, p_col, 0.0), axis=0, keepdims=True)
    c_col = jnp.sum(jnp.where(i1 < i0, p_wide, 0.0), axis=1, keepdims=True)
    rank_row = jnp.sum(jnp.where((i0 < i1) & same, p_col, 0.0), axis=0, keepdims=True)
    rank_col = jnp.sum(jnp.where((i1 < i0) & same, p_wide, 0.0), axis=1, keepdims=True)
    slot_row = t_row * 2.0 + rank_row
    slot_col = t_col * 2.0 + rank_col

    def hot(values, on, shape, dim):
        ids = lax.broadcasted_iota(jnp.int32, shape, dim).astype(F32)
        return jnp.where(values == ids, on, 0.0)

    pick_f = hot(c_row, p_row, (8, n), 0)
    pick = pick_f.astype(BF16)
    pick_t = hot(c_col, p_col, (n, 8), 1).astype(BF16)
    slots = hot(slot_row, p_row, (16, n), 0).astype(BF16)
    slots_t = hot(slot_col, p_col, (n, 16), 1).astype(BF16)
    place = mm(slots, pick_t).astype(BF16)
    place_t = mm(pick, slots_t).astype(BF16)
    gate_tok = jax.nn.sigmoid(score[...]).astype(BF16).astype(F32)
    gate = jnp.sum(pick_f * gate_tok, axis=1, keepdims=True)
    rows_g[0, 0] = mm(pick, merged[...]).astype(BF16)
    cot_send[...] = cot_in[...].reshape(8, 2, cot_in.shape[1])

    pl.semaphore_wait(barrier, len(peers))

    def gather(k, buf):
        send_z, send_y = ag_send.at[k, 0], ag_send.at[k, 1]

        def z_one(slot, back, dist):
            push(buf.at[0, slot], buf.at[0, back], send_z, ag_zrecv.at[k, back], at_z(dist))

        def first():
            for d in (4, 3, 2, 1):
                z_one(0, 16 - d, d)
                z_one(0, d, -d)

        def second():
            got(buf.at[0, 12], ag_zrecv.at[k, 12])
            for d in (4, 3, 2, 1):
                z_one(12, 12 - d, d)
            got(buf.at[0, 4], ag_zrecv.at[k, 4])
            for d in (3, 2, 1):
                z_one(4, 4 + d, -d)

        def spread(g):
            lo, hi = GROUPS[g]
            for s in range(lo, hi):
                if s not in (0, 4, 12):
                    got(buf.at[0, s], ag_zrecv.at[k, s])
            r = pl.ds(lo, hi - lo)
            push(buf.at[0, r], buf.at[3, r], send_y, ag_yrecv.at[k, 3, g], at_y(1))
            push(buf.at[0, r], buf.at[1, r], send_y, ag_yrecv.at[k, 1, g], at_y(-1))

        def relay_on(g):
            lo, hi = GROUPS[g]
            r = pl.ds(lo, hi - lo)
            q, to = (1, -1) if g in (NEAR_M, FAR_M) else (3, 1)
            got(buf.at[q, r], ag_yrecv.at[k, q, g])
            push(buf.at[q, r], buf.at[2, r], send_y, ag_yrecv.at[k, 2, g], at_y(to))

        def finish():
            for g, (lo, hi) in enumerate(GROUPS):
                r = pl.ds(lo, hi - lo)
                q = 3 if g in (NEAR_M, FAR_M) else 1
                got(buf.at[q, r], ag_yrecv.at[k, q, g])
                got(buf.at[2, r], ag_yrecv.at[k, 2, g])

        def drain():
            sent(buf.at[0, pl.ds(0, 15)], send_z)
            sent(buf.at[pl.ds(0, 3)], send_y)

        return first, second, spread, relay_on, finish, drain

    def hidden_sum(k):
        def exchange(value):
            part[k] = value.reshape(part.shape[1:])
            push(part.at[k, 1 - core], part_in.at[k], x_sem.at[k, 0], x_sem.at[k, 1], partner)

        def scatter():
            got(part_in.at[k], x_sem.at[k, 1])
            share[k] = part[k, core] + part_in[k]
            for j in (2, 1, 3):
                push(
                    share.at[k, (x + j) % 4], share_in.at[k, j - 1],
                    x_sem.at[k, 2], x_sem.at[k, 3], at_x(j),
                )

        def total():
            got(share_in.at[k], x_sem.at[k, 3])
            return share[k, x] + share_in[k, 0] + share_in[k, 1] + share_in[k, 2]

        def widen(buf, value):
            buf[core * 4 + x] = value.astype(BF16)
            mine = buf.at[core * 4 + x]
            for j in (4, 5, 2, 3, 6, 7, 1):
                push(mine, mine, x_sem.at[k, 4], x_sem.at[k, 5], at_ten(j))

        def widened(buf):
            got(buf.at[pl.ds(0, 7)], x_sem.at[k, 5])
            return buf[...].reshape(-1, buf.shape[-1])

        def drain():
            sent(part_in.at[k], x_sem.at[k, 0])
            sent(share_in.at[k], x_sem.at[k, 2])
            sent(act_g.at[pl.ds(0, 7)], x_sem.at[k, 4])

        return exchange, scatter, total, widen, widened, drain

    def reduce_rows(k):
        t, yi, r16 = terms.at[k], y_in.at[k], rb.at[k]
        send_y, send_z = rs_send.at[k, 0], rs_send.at[k, 1]
        plus, minus = {0: (5, 8), 1: (0, 5)}, {0: (8, 12), 1: (12, 16)}

        def y_push(kind, q, lo, hi, to, f):
            r = pl.ds(lo, hi - lo)
            s = pl.ds(lo % 8, hi - lo)
            push(t.at[q, r], yi.at[kind, s], send_y, rs_yrecv.at[k, kind, f], at_y(to))

        def y_got(kind, lo, hi, f):
            got(yi.at[kind, pl.ds(lo % 8, hi - lo)], rs_yrecv.at[k, kind, f])

        def start(value):
            terms[k] = value.astype(BF16).reshape(terms.shape[1:])
            for f in (0, 1):
                y_push(0, 2, *plus[f], 1, f)
                y_push(1, 2, *minus[f], -1, f)
                y_push(2, 3, *plus[f], -1, f)
                y_push(3, 1, *minus[f], 1, f)

        def add(q, lo, hi, kind):
            return t[q, lo:hi].astype(F32) + yi[kind, lo % 8 : lo % 8 + hi - lo].astype(F32)

        def y_second(f):
            lo, hi = plus[f]
            y_got(0, lo, hi, f)
            t[1, lo:hi] = add(1, lo, hi, 0).astype(BF16)
            y_push(4, 1, lo, hi, 1, f)
            lo, hi = minus[f]
            y_got(1, lo, hi, f)
            t[3, lo:hi] = add(3, lo, hi, 1).astype(BF16)
            y_push(5, 3, lo, hi, -1, f)

        def y_end(f):
            for kinds, (lo, hi) in (((2, 4), plus[f]), ((3, 5), minus[f])):
                for kind in kinds:
                    y_got(kind, lo, hi, f)
                both = add(0, lo, hi, kinds[0]) + yi[kinds[1], lo % 8 : lo % 8 + hi - lo].astype(F32)
                rf[k, lo:hi] = both
                rb[k, lo:hi] = both.astype(BF16)

        def z_far():
            y_end(0)
            for d in (4, 3, 2, 1):
                push(r16.at[4 + d], far_p.at[k, d - 1], send_z, rs_zrecv.at[k, 0], at_z(d))
            for d in (3, 2, 1):
                push(r16.at[12 - d], far_m.at[k, d - 1], send_z, rs_zrecv.at[k, 1], at_z(-d))

        def z_near():
            y_end(1)
            for d in (3, 2, 1):
                push(r16.at[d], fin.at[k, d - 1], send_z, rs_zrecv.at[k, 2], at_z(d))
                push(r16.at[16 - d], fin.at[k, d + 2], send_z, rs_zrecv.at[k, 2], at_z(-d))

        def z_relay():
            got(far_p.at[k], rs_zrecv.at[k, 0])
            total = rf[k, 4]
            for d in range(4):
                total += far_p[k, d].astype(F32)
            relay[k, 0] = total.astype(BF16)
            push(relay.at[k, 0], fin.at[k, 6], send_z, rs_zrecv.at[k, 2], at_z(4))
            got(far_m.at[k], rs_zrecv.at[k, 1])
            total = rf[k, 12]
            for d in range(3):
                total += far_m[k, d].astype(F32)
            relay[k, 1] = total.astype(BF16)
            push(relay.at[k, 1], fin.at[k, 7], send_z, rs_zrecv.at[k, 2], at_z(-4))

        def result():
            got(fin.at[k], rs_zrecv.at[k, 2])
            total = rf[k, 0]
            for d in range(8):
                total += fin[k, d].astype(F32)
            return total

        def drain():
            sent(t.at[pl.ds(0, 3)], send_y)
            sent(r16.at[pl.ds(0, 15)], send_z)

        return start, y_second, z_far, z_near, z_relay, result, drain

    def seq_send(k, src, dst):
        for j in (7, 6, 5, 4, 3, 2, 1):
            push(src.at[(seq + j) % 8], dst.at[seq], a_sem.at[k, 0], a_sem.at[k, 1], at_seq(j))
        dst[seq] = src[seq]

    def seq_got(k, dst):
        got(dst.at[pl.ds(0, 7)], a_sem.at[k, 1])
        return dst[...].reshape(16, dst.shape[-1])

    r_first, r_second, r_spread, r_relay, r_finish, r_drain = gather(0, rows_g)
    s_first, s_second, s_spread, s_relay, s_finish, s_drain = gather(1, scaled_g)
    h0 = hidden_sum(0)
    h1 = hidden_sum(1)
    y0 = reduce_rows(0)
    y1 = reduce_rows(1)

    r_first()
    seq_send(0, cot_send, cot_recv)
    r_spread(OWN)
    r_second()
    r_spread(NEAR_P)
    r_spread(NEAR_M)
    r_relay(OWN)
    cot = mm(place_t, seq_got(0, cot_recv))
    scaled_g[0, 0] = (gate * cot).astype(BF16)
    s_first()
    s_spread(OWN)
    r_relay(NEAR_P)
    r_relay(NEAR_M)
    r_spread(FAR_M)
    r_spread(FAR_P)
    s_second()
    r_relay(FAR_M)
    r_relay(FAR_P)
    s_relay(OWN)
    s_spread(NEAR_P)
    s_spread(NEAR_M)
    r_finish()
    load_up.wait()
    every_row = rows_g[...].reshape(512, -1)
    h0[0](mm(every_row, up_w[...]))
    s_spread(FAR_M)
    s_spread(FAR_P)
    s_relay(NEAR_P)
    s_relay(NEAR_M)
    h0[1]()
    s_relay(FAR_M)
    s_relay(FAR_P)
    pre = h0[2]()
    sig = jax.nn.sigmoid(pre)
    h0[3](act_g, pre * sig)
    s_finish()
    load_down.wait()
    every_scaled = scaled_g[...].reshape(512, -1)
    h1[0](mm(every_scaled, down_w[...], 1, 1))
    act = h0[4](act_g)
    y0[0](mm(act, down_w[...]))
    h1[1]()
    y0[1](0)
    act_grad = h1[2]()
    h1[3](pg_g, act_grad * sig * (1.0 + pre * (1.0 - sig)))
    y0[1](1)
    y0[2]()
    pre_grad = h1[4](pg_g)
    y1[0](mm(pre_grad, up_w[...], 1, 1))
    y0[3]()
    down_acc[...] = mm(act, every_scaled, 0, 0)
    store_down = pltpu.make_async_copy(down_acc, down_out, local_sem.at[2])
    store_down.start()
    y0[4]()
    y1[1](0)
    y1[1](1)
    y1[2]()
    up_acc[...] = mm(every_row, pre_grad, 0, 0)
    store_up = pltpu.make_async_copy(up_acc, up_out, local_sem.at[3])
    store_up.start()
    mixed = (rows_g[0, 0].astype(F32) + gate * y0[5]()).astype(BF16)
    mix_send[...] = mm(place, mixed).astype(BF16).reshape(mix_send.shape)
    seq_send(1, mix_send, mix_recv)
    y1[3]()
    y1[4]()
    slot_grad = (cot + y1[5]()).astype(BF16)
    token_out[...] = mm(pick_t, slot_grad).astype(BF16)
    mixed_out[...] = seq_got(1, mix_recv)

    store_down.wait()
    store_up.wait()
    r_drain()
    s_drain()
    h0[5]()
    h1[5]()
    y0[6]()
    y1[6]()
    sent(cot_recv.at[pl.ds(0, 7)], a_sem.at[0, 0])
    sent(mix_recv.at[pl.ds(0, 7)], a_sem.at[1, 0])


def per_device(merged, positions, picked, router_score, up_weight, down_weight, mixed_grad):
    width = merged.shape[1]
    hidden = up_weight.shape[1]
    vmem = pl.BlockSpec(memory_space=pltpu.VMEM)
    hbm = pl.BlockSpec(memory_space=pl.ANY)
    dma = pltpu.SemaphoreType.DMA
    block = (8, width)
    return pl.pallas_call(
        kernel,
        name="routed_ffn",
        out_shape=(
            jax.ShapeDtypeStruct(mixed_grad.shape, BF16),
            jax.ShapeDtypeStruct(merged.shape, BF16),
            jax.ShapeDtypeStruct(up_weight.shape, F32),
            jax.ShapeDtypeStruct(down_weight.shape, F32),
        ),
        in_specs=[vmem] * 5 + [hbm] * 2,
        out_specs=(vmem, vmem, hbm, hbm),
        scratch_shapes=[
            pltpu.VMEM(up_weight.shape, BF16),
            pltpu.VMEM(down_weight.shape, BF16),
            pltpu.VMEM((4, 16, *block), BF16),
            pltpu.VMEM((4, 16, *block), BF16),
            pltpu.VMEM((2, 2, 4, 64, hidden), F32),
            pltpu.VMEM((2, 4, 64, hidden), F32),
            pltpu.VMEM((2, 4, 64, hidden), F32),
            pltpu.VMEM((2, 3, 64, hidden), F32),
            pltpu.VMEM((8, 64, hidden), BF16),
            pltpu.VMEM((8, 64, hidden), BF16),
            pltpu.VMEM((2, 4, 16, *block), BF16),
            pltpu.VMEM((2, 6, 8, *block), BF16),
            pltpu.VMEM((2, 16, *block), BF16),
            pltpu.VMEM((2, 16, *block), F32),
            pltpu.VMEM((2, 4, *block), BF16),
            pltpu.VMEM((2, 3, *block), BF16),
            pltpu.VMEM((2, 8, *block), BF16),
            pltpu.VMEM((2, 2, *block), BF16),
            pltpu.VMEM((8, 2, width), BF16),
            pltpu.VMEM((8, 2, width), BF16),
            pltpu.VMEM((8, 2, width), BF16),
            pltpu.VMEM((8, 2, width), BF16),
            pltpu.VMEM(up_weight.shape, F32),
            pltpu.VMEM(down_weight.shape, F32),
            dma((4,)),
            dma((2, 16)),
            dma((2, 4, 5)),
            dma((2, 2)),
            dma((2, 6, 2)),
            dma((2, 3)),
            dma((2, 2)),
            dma((2, 6)),
            dma((2, 2)),
        ],
        compiler_params=pltpu.CompilerParams(
            collective_id=0, has_side_effects=True, vmem_limit_bytes=48 * 1024 * 1024
        ),
    )(
        merged,
        positions.reshape(1, -1),
        picked.reshape(1, -1),
        router_score.reshape(1, -1),
        mixed_grad,
        up_weight,
        down_weight,
    )


def solution(mesh):
    placed = (
        P(VIT_SEQ, "tensor"),
        P(VIT_SEQ),
        P(VIT_SEQ),
        P(VIT_SEQ),
        P("tensor", VIT_SEQ),
        P(VIT_SEQ, "tensor"),
        P(VIT_SEQ, "tensor"),
    )
    return jax.shard_map(
        per_device,
        mesh=mesh,
        in_specs=placed,
        out_specs=(
            P(VIT_SEQ, "tensor"),
            P(VIT_SEQ, "tensor"),
            P("tensor", VIT_SEQ),
            P(VIT_SEQ, "tensor"),
        ),
        check_vma=False,
    )
```

time: 496 us -> 90.1 us (0.18)
  waiting for transfers between devices: 242 us -> 0 us
  blocking collectives: 132 us -> 0 us
  Pallas kernels: 0 us -> 80.4 us
  starting transfers between devices: 68.6 us -> 0 us
  matrix products: 16.6 us -> 0 us
  between operations: 14.2 us -> 0.67 us
  other arithmetic: 10.4 us -> 0 us
    all_to_all x7 -> x0, waiting for transfers between devices: 216 us -> none  [the longest x2 180 us: row_sum(): lax.all_to_all(pieces, VIT_SEQ, split_axis=0, concat_axis=0, tiled=True)]
    all_gather x4 -> x0, blocking collectives: 119 us -> none  [gather_in_order(): parts = lax.all_gather(parts, axes[k])]
    pallas_call x0 -> x1, Pallas kernels: none -> 80.4 us  [per_device(): pl.pallas_call(kernel, name='routed_ffn', out_shape=(jax.ShapeDtypeStruct...]
    all_to_all x7 -> x0, starting transfers between devices: 68.6 us -> none  [the longest x2 26.4 us: sum_at_owner(): lax.all_to_all(parts, axis, split_axis=0, concat_axis=0, tiled=True)]
    all_gather x2 -> x0, waiting for transfers between devices: 25.7 us -> none  [gather_in_order(): parts = lax.all_gather(parts, axes[k])]
    dot_general x9 -> x0, matrix products: 16.6 us -> none  [the longest x2 5.32 us: row_sum(): lax.dot_general(left, right, (((1,), (contract,)), ((), ())), preferred_e...]
    all_to_all x1 -> x0, blocking collectives: 12.7 us -> none  [sent_to_all(): lax.all_to_all(jnp.broadcast_to(x[None], (count, *x.shape)), axis, 0, 0,...]
    reduce_sum x5 -> x0, other arithmetic: 7.34 us -> none  [the longest x2 3.9 us: row_sum(): return jnp.sum(arrived.astype(jnp.float32), axis=0)]
  transfers between devices with their start and end apart: 9 -> 0, of which waited for: 7 -> 0; matrix products, arithmetic and copies ran while one was open for 5% -> 0% of each run, Pallas kernels for 0% -> 0%
where the time goes in v1:
time: 90.1 us; the launch traced here: 88.6 us
  Pallas kernels  80.4 us (89%)
  local copies, waits for them, and re-layouts  7.53 us (8%)
    pallas_call x1, Pallas kernels, per_device(): pl.pallas_call(kernel, name='routed_ffn', out_shape=(jax.ShapeDtypeStruct...  80.4 us
    unnamed x18, local copies, waits for them, and re-layouts  7.53 us

profile of v1, /device:TPU:1, one launch (start us, length us, event | category | flops | bytes accessed | tf_op | source)
XLA Modules:
  0.0 88.6 jit_solution(15449275954141524837)
XLA Ops:
  0.6 0.0 copy-start.4
  0.6 0.0 copy-start.5
  0.7 0.0 copy-start.6
  0.7 0.6 copy-done.4
  1.3 0.0 copy-done.5
  1.3 0.0 copy-done.6
  1.3 0.0 copy-start
  1.3 1.0 %copy-done = bf16[1024,256]{1,0:T(8,128)(2,1)S(1)} copy-done((bf16[1024,256]{1,0:T(8,128)(2,1)S(1)}, bf16[1024,256]{1,0:T(8,128)(2,1)}, u32[]{:S(2)}) %copy-start) | copy-done | bytes 524312
  2.4 0.0 copy-start.1
  2.4 1.0 %copy-done.1 = bf16[256,1024]{1,0:T(8,128)(2,1)S(1)} copy-done((bf16[256,1024]{1,0:T(8,128)(2,1)S(1)}, bf16[256,1024]{1,0:T(8,128)(2,1)}, u32[]{:S(2)}) %copy-start.1) | copy-done | bytes 524312
  3.4 0.0 copy-start.2
  3.4 0.8 copy-done.2
  4.2 0.0 copy-start.3
  4.2 0.8 copy-done.3
  5.0 80.4 %routed_ffn.1 = (bf16[16,1024]{1,0:T(8,128)(2,1)S(1)}, bf16[32,1024]{1,0:T(8,128)(2,1)S(1)}, f32[1024,256]{1,0:T(8,128)S(1)}, f32[256,1024]{1,0:T(8,128)S(1)}) custom-call(bf16[32,1024]{1,0:T(8,128)(2,1)S(1)} %copy-done.2, s32[1,32]{1,0:T(1,128)S(1)} %bitcast.3, s32[1,32]{1,0:T(1,128)S(1)} %bitcast.4, f32[1,32]{1,0:T(1,128)S(1)} %bitcast.5, ...), custom_call_target="tpu_custom_call" | custom-call | tf_op jit(solution)/shard_map/routed_ffn/pallas_call | solution.py:386
  85.5 0.6 copy.15
  86.1 0.6 copy.16
  86.7 1.0 %copy.17 = f32[1024,256]{1,0:T(8,128)} copy(f32[1024,256]{1,0:T(8,128)S(1)} %get-tuple-element.10) | data formatting | bytes 2097152
  87.7 1.0 %copy.18 = f32[256,1024]{1,0:T(8,128)} copy(f32[256,1024]{1,0:T(8,128)S(1)} %get-tuple-element.11) | data formatting | bytes 2097152
Async XLA Ops:
  0.6 0.7 copy-start.4
  0.6 0.7 copy-start.5
  0.7 0.7 copy-start.6
  1.3 1.0 %copy-start = (bf16[1024,256]{1,0:T(8,128)(2,1)S(1)}, bf16[1024,256]{1,0:T(8,128)(2,1)}, u32[]{:S(2)}) copy-start(bf16[1024,256]{1,0:T(8,128)(2,1)} %up_hbm.1) | copy-start | bytes 1572868
  2.4 1.0 %copy-start.1 = (bf16[256,1024]{1,0:T(8,128)(2,1)S(1)}, bf16[256,1024]{1,0:T(8,128)(2,1)}, u32[]{:S(2)}) copy-start(bf16[256,1024]{1,0:T(8,128)(2,1)} %down_hbm.1) | copy-start | bytes 1572868
  3.4 0.8 copy-start.2
  4.2 0.8 copy-start.3

commit v2 on v1

--- a/solution.py
+++ b/solution.py
@@ -21,11 +21,12 @@
 
 
 def kernel(
-    merged, pos, picked, score, cot_in, up_hbm, down_hbm,
+    merged_hbm, pos_hbm, picked_hbm, score_hbm, cot_hbm, up_hbm, down_hbm,
+    mixed_hbm, token_hbm, up_grad_hbm, down_grad_hbm,
+    merged, pos, picked, score, cot_in, up_w, down_w, rows_g, scaled_g, part, part_in, share, share_in, act_g, pg_g,
+    terms, y_in, rb, rf, far_p, far_m, fin, relay,
+    cot_send, cot_recv, mix_send, mix_recv, share_f,
     mixed_out, token_out, up_out, down_out,
-    up_w, down_w, rows_g, scaled_g, part, part_in, share, share_in, act_g, pg_g,
-    terms, y_in, rb, rf, far_p, far_m, fin, relay,
-    cot_send, cot_recv, mix_send, mix_recv, up_acc, down_acc,
     local_sem, ag_zrecv, ag_yrecv, ag_send, rs_yrecv, rs_zrecv, rs_send, x_sem, a_sem,
 ):
     vit, seq, ten = (lax.axis_index(a) for a in ("vit", "seq", "tensor"))
@@ -65,10 +66,27 @@
     def sent(src, send):
         remote(src, src, send, send, partner).wait_send()
 
-    load_up = pltpu.make_async_copy(up_hbm, up_w, local_sem.at[0])
-    load_down = pltpu.make_async_copy(down_hbm, down_w, local_sem.at[1])
-    load_up.start()
-    load_down.start()
+    loads = [
+        pltpu.make_async_copy(src, dst, local_sem.at[i])
+        for i, (src, dst) in enumerate(
+            (
+                (pos_hbm, pos), (picked_hbm, picked), (merged_hbm, merged), (cot_hbm, cot_in),
+                (score_hbm, score), (up_hbm, up_w), (down_hbm, down_w),
+            )
+        )
+    ]
+    for load in loads:
+        load.start()
+
+    stores = [
+        pltpu.make_async_copy(src, dst, local_sem.at[7 + i])
+        for i, (src, dst) in enumerate(
+            (
+                (mixed_out, mixed_hbm), (token_out, token_hbm),
+                (up_out, up_grad_hbm), (down_out, down_grad_hbm),
+            )
+        )
+    ]
 
     barrier = pltpu.get_barrier_semaphore()
     peers = [at_z(k) for k in (4, -4, 3, -3, 2, -2, 1, -1)]
@@ -79,40 +97,48 @@
         pl.semaphore_signal(barrier, inc=1, device_id=peer, device_id_type=MESH)
 
     n = pos.shape[1]
-    t_row = (pos[...] >> 14).astype(F32)
-    p_row = picked[...].astype(F32)
     i0 = lax.broadcasted_iota(jnp.int32, (n, n), 0)
     i1 = lax.broadcasted_iota(jnp.int32, (n, n), 1)
     eye = i0 == i1
-    t_wide = jnp.broadcast_to(t_row, (n, n))
-    p_wide = jnp.broadcast_to(p_row, (n, n))
-    t_col = jnp.sum(jnp.where(eye, t_wide, 0.0), axis=1, keepdims=True)
-    p_col = jnp.sum(jnp.where(eye, p_wide, 0.0), axis=1, keepdims=True)
-    same = t_col == t_wide
-    c_row = jnp.sum(jnp.where(i0 < i1, p_col, 0.0), axis=0, keepdims=True)
-    c_col = jnp.sum(jnp.where(i1 < i0, p_wide, 0.0), axis=1, keepdims=True)
-    rank_row = jnp.sum(jnp.where((i0 < i1) & same, p_col, 0.0), axis=0, keepdims=True)
-    rank_col = jnp.sum(jnp.where((i1 < i0) & same, p_wide, 0.0), axis=1, keepdims=True)
-    slot_row = t_row * 2.0 + rank_row
-    slot_col = t_col * 2.0 + rank_col
 
     def hot(values, on, shape, dim):
         ids = lax.broadcasted_iota(jnp.int32, shape, dim).astype(F32)
         return jnp.where(values == ids, on, 0.0)
 
+    loads[1].wait()
+    p_row = picked[...].astype(F32)
+    p_wide = jnp.broadcast_to(p_row, (n, n))
+    p_col = jnp.sum(jnp.where(eye, p_wide, 0.0), axis=1, keepdims=True)
+    c_row = jnp.sum(jnp.where(i0 < i1, p_col, 0.0), axis=0, keepdims=True)
     pick_f = hot(c_row, p_row, (8, n), 0)
     pick = pick_f.astype(BF16)
-    pick_t = hot(c_col, p_col, (n, 8), 1).astype(BF16)
-    slots = hot(slot_row, p_row, (16, n), 0).astype(BF16)
-    slots_t = hot(slot_col, p_col, (n, 16), 1).astype(BF16)
-    place = mm(slots, pick_t).astype(BF16)
-    place_t = mm(pick, slots_t).astype(BF16)
-    gate_tok = jax.nn.sigmoid(score[...]).astype(BF16).astype(F32)
-    gate = jnp.sum(pick_f * gate_tok, axis=1, keepdims=True)
+    loads[2].wait()
     rows_g[0, 0] = mm(pick, merged[...]).astype(BF16)
+    loads[3].wait()
     cot_send[...] = cot_in[...].reshape(8, 2, cot_in.shape[1])
 
     pl.semaphore_wait(barrier, len(peers))
+
+    def routing():
+        loads[0].wait()
+        t_row = (pos[...] >> 14).astype(F32)
+        t_wide = jnp.broadcast_to(t_row, (n, n))
+        t_col = jnp.sum(jnp.where(eye, t_wide, 0.0), axis=1, keepdims=True)
+        same = t_col == t_wide
+        c_col = jnp.sum(jnp.where(i1 < i0, p_wide, 0.0), axis=1, keepdims=True)
+        rank_row = jnp.sum(jnp.where((i0 < i1) & same, p_col, 0.0), axis=0, keepdims=True)
+        rank_col = jnp.sum(jnp.where((i1 < i0) & same, p_wide, 0.0), axis=1, keepdims=True)
+        slot_row = t_row * 2.0 + rank_row
+        slot_col = t_col * 2.0 + rank_col
+        pick_t = hot(c_col, p_col, (n, 8), 1).astype(BF16)
+        slots = hot(slot_row, p_row, (16, n), 0).astype(BF16)
+        slots_t = hot(slot_col, p_col, (n, 16), 1).astype(BF16)
+        place = mm(slots, pick_t).astype(BF16)
+        place_t = mm(pick, slots_t).astype(BF16)
+        loads[4].wait()
+        gate_tok = jax.nn.sigmoid(score[...]).astype(BF16).astype(F32)
+        gate = jnp.sum(pick_f * gate_tok, axis=1, keepdims=True)
+        return pick_t, place, place_t, gate
 
     def gather(k, buf):
         send_z, send_y = ag_send.at[k, 0], ag_send.at[k, 1]
@@ -169,7 +195,9 @@
 
         def scatter():
             got(part_in.at[k], x_sem.at[k, 1])
-            share[k] = part[k, core] + part_in[k]
+            both = part[k, core] + part_in[k]
+            share_f[k] = both
+            share[k] = both.astype(BF16)
             for j in (2, 1, 3):
                 push(
                     share.at[k, (x + j) % 4], share_in.at[k, j - 1],
@@ -178,24 +206,31 @@
 
         def total():
             got(share_in.at[k], x_sem.at[k, 3])
-            return share[k, x] + share_in[k, 0] + share_in[k, 1] + share_in[k, 2]
+            arrived = share_in[k].astype(F32)
+            return share_f[k, x] + arrived[0] + arrived[1] + arrived[2]
 
         def widen(buf, value):
             buf[core * 4 + x] = value.astype(BF16)
             mine = buf.at[core * 4 + x]
-            for j in (4, 5, 2, 3, 6, 7, 1):
-                push(mine, mine, x_sem.at[k, 4], x_sem.at[k, 5], at_ten(j))
+            for j in (2, 1, 3):
+                push(mine, mine, x_sem.at[k, 4], x_sem.at[k, 5], at_x(j))
+
+        def pair(buf):
+            got(buf.at[pl.ds(0, 3)], x_sem.at[k, 5])
+            half = buf.at[pl.ds(core * 4, 4)]
+            push(half, half, x_sem.at[k, 6], x_sem.at[k, 7], partner)
 
         def widened(buf):
-            got(buf.at[pl.ds(0, 7)], x_sem.at[k, 5])
+            got(buf.at[pl.ds(0, 4)], x_sem.at[k, 7])
             return buf[...].reshape(-1, buf.shape[-1])
 
         def drain():
             sent(part_in.at[k], x_sem.at[k, 0])
             sent(share_in.at[k], x_sem.at[k, 2])
-            sent(act_g.at[pl.ds(0, 7)], x_sem.at[k, 4])
-
-        return exchange, scatter, total, widen, widened, drain
+            sent(act_g.at[pl.ds(0, 3)], x_sem.at[k, 4])
+            sent(act_g.at[pl.ds(0, 4)], x_sem.at[k, 6])
+
+        return exchange, scatter, total, widen, pair, widened, drain
 
     def reduce_rows(k):
         t, yi, r16 = terms.at[k], y_in.at[k], rb.at[k]
@@ -215,8 +250,13 @@
             for f in (0, 1):
                 y_push(0, 2, *plus[f], 1, f)
                 y_push(1, 2, *minus[f], -1, f)
-                y_push(2, 3, *plus[f], -1, f)
-                y_push(3, 1, *minus[f], 1, f)
+                if f == 0:
+                    y_push(2, 3, *plus[f], -1, f)
+                    y_push(3, 1, *minus[f], 1, f)
+
+        def start_near():
+            y_push(2, 3, *plus[1], -1, 1)
+            y_push(3, 1, *minus[1], 1, 1)
 
         def add(q, lo, hi, kind):
             return t[q, lo:hi].astype(F32) + yi[kind, lo % 8 : lo % 8 + hi - lo].astype(F32)
@@ -277,7 +317,7 @@
             sent(t.at[pl.ds(0, 3)], send_y)
             sent(r16.at[pl.ds(0, 15)], send_z)
 
-        return start, y_second, z_far, z_near, z_relay, result, drain
+        return start, start_near, y_second, z_far, z_near, z_relay, result, drain
 
     def seq_send(k, src, dst):
         for j in (7, 6, 5, 4, 3, 2, 1):
@@ -295,95 +335,127 @@
     y0 = reduce_rows(0)
     y1 = reduce_rows(1)
 
+    h0_exchange, h0_scatter, h0_total, h0_widen, h0_pair, h0_widened, h0_drain = h0
+    h1_exchange, h1_scatter, h1_total, h1_widen, h1_pair, h1_widened, h1_drain = h1
+    y0_start, y0_near, y0_second, y0_z_far, y0_z_near, y0_z_relay, y0_result, y0_drain = y0
+    y1_start, y1_near, y1_second, y1_z_far, y1_z_near, y1_z_relay, y1_result, y1_drain = y1
+
+    seq_send(0, cot_send, cot_recv)
     r_first()
-    seq_send(0, cot_send, cot_recv)
     r_spread(OWN)
+    pick_t, place, place_t, gate = routing()
     r_second()
     r_spread(NEAR_P)
     r_spread(NEAR_M)
-    r_relay(OWN)
     cot = mm(place_t, seq_got(0, cot_recv))
     scaled_g[0, 0] = (gate * cot).astype(BF16)
     s_first()
     s_spread(OWN)
+    r_relay(OWN)
     r_relay(NEAR_P)
     r_relay(NEAR_M)
     r_spread(FAR_M)
     r_spread(FAR_P)
     s_second()
+    s_relay(OWN)
     r_relay(FAR_M)
     r_relay(FAR_P)
-    s_relay(OWN)
     s_spread(NEAR_P)
     s_spread(NEAR_M)
     r_finish()
-    load_up.wait()
+    loads[5].wait()
     every_row = rows_g[...].reshape(512, -1)
-    h0[0](mm(every_row, up_w[...]))
+    h0_exchange(mm(every_row, up_w[...]))
     s_spread(FAR_M)
     s_spread(FAR_P)
     s_relay(NEAR_P)
     s_relay(NEAR_M)
-    h0[1]()
+    h0_scatter()
     s_relay(FAR_M)
     s_relay(FAR_P)
-    pre = h0[2]()
+    pre = h0_total()
     sig = jax.nn.sigmoid(pre)
-    h0[3](act_g, pre * sig)
+    h0_widen(act_g, pre * sig)
     s_finish()
-    load_down.wait()
+    loads[6].wait()
     every_scaled = scaled_g[...].reshape(512, -1)
-    h1[0](mm(every_scaled, down_w[...], 1, 1))
-    act = h0[4](act_g)
-    y0[0](mm(act, down_w[...]))
-    h1[1]()
-    y0[1](0)
-    act_grad = h1[2]()
-    h1[3](pg_g, act_grad * sig * (1.0 + pre * (1.0 - sig)))
-    y0[1](1)
-    y0[2]()
-    pre_grad = h1[4](pg_g)
-    y1[0](mm(pre_grad, up_w[...], 1, 1))
-    y0[3]()
-    down_acc[...] = mm(act, every_scaled, 0, 0)
-    store_down = pltpu.make_async_copy(down_acc, down_out, local_sem.at[2])
-    store_down.start()
-    y0[4]()
-    y1[1](0)
-    y1[1](1)
-    y1[2]()
-    up_acc[...] = mm(every_row, pre_grad, 0, 0)
-    store_up = pltpu.make_async_copy(up_acc, up_out, local_sem.at[3])
-    store_up.start()
-    mixed = (rows_g[0, 0].astype(F32) + gate * y0[5]()).astype(BF16)
+    h1_exchange(mm(every_scaled, down_w[...], 1, 1))
+    h0_pair(act_g)
+    h1_scatter()
+    act = h0_widened(act_g)
+    y0_start(mm(act, down_w[...]))
+    act_grad = h1_total()
+    h1_widen(pg_g, act_grad * sig * (1.0 + pre * (1.0 - sig)))
+    y0_second(0)
+    y0_near()
+    h1_pair(pg_g)
+    y0_second(1)
+    y0_z_far()
+    pre_grad = h1_widened(pg_g)
+    y1_start(mm(pre_grad, up_w[...], 1, 1))
+    y0_z_near()
+    down_out[...] = mm(act, every_scaled, 0, 0)
+    stores[3].start()
+    y1_second(0)
+    y1_near()
+    y0_z_relay()
+    y1_second(1)
+    y1_z_far()
+    up_out[...] = mm(every_row, pre_grad, 0, 0)
+    stores[2].start()
+    y1_z_near()
+    mixed = (rows_g[0, 0].astype(F32) + gate * y0_result()).astype(BF16)
     mix_send[...] = mm(place, mixed).astype(BF16).reshape(mix_send.shape)
     seq_send(1, mix_send, mix_recv)
-    y1[3]()
-    y1[4]()
-    slot_grad = (cot + y1[5]()).astype(BF16)
+    y1_z_relay()
+    slot_grad = (cot + y1_result()).astype(BF16)
     token_out[...] = mm(pick_t, slot_grad).astype(BF16)
+    stores[1].start()
     mixed_out[...] = seq_got(1, mix_recv)
-
-    store_down.wait()
-    store_up.wait()
+    stores[0].start()
+
     r_drain()
     s_drain()
-    h0[5]()
-    h1[5]()
-    y0[6]()
-    y1[6]()
+    h0_drain()
+    h1_drain()
+    y0_drain()
+    y1_drain()
     sent(cot_recv.at[pl.ds(0, 7)], a_sem.at[0, 0])
     sent(mix_recv.at[pl.ds(0, 7)], a_sem.at[1, 0])
+    for store in stores:
+        store.wait()
+
+
+def put_out(*refs):
+    ins, outs, bufs, sem = refs[:4], refs[4:8], refs[8:12], refs[12]
+    pieces = []
+    for i, count in ((2, 4), (3, 4), (0, 1), (1, 1)):
+        rows = ins[i].shape[0] // count
+        for j in range(count):
+            part = pl.ds(j * rows, rows)
+            n = len(pieces)
+            pieces.append(
+                (
+                    pltpu.make_async_copy(ins[i].at[part], bufs[i].at[part], sem.at[0, n]),
+                    pltpu.make_async_copy(bufs[i].at[part], outs[i].at[part], sem.at[1, n]),
+                )
+            )
+    for taken, _ in pieces:
+        taken.start()
+    for taken, put in pieces:
+        taken.wait()
+        put.start()
+    for _, put in pieces:
+        put.wait()
 
 
 def per_device(merged, positions, picked, router_score, up_weight, down_weight, mixed_grad):
     width = merged.shape[1]
     hidden = up_weight.shape[1]
-    vmem = pl.BlockSpec(memory_space=pltpu.VMEM)
-    hbm = pl.BlockSpec(memory_space=pl.ANY)
+    hbm = pl.BlockSpec(memory_space=pltpu.HBM)
     dma = pltpu.SemaphoreType.DMA
     block = (8, width)
-    return pl.pallas_call(
+    results = pl.pallas_call(
         kernel,
         name="routed_ffn",
         out_shape=(
@@ -392,17 +464,22 @@
             jax.ShapeDtypeStruct(up_weight.shape, F32),
             jax.ShapeDtypeStruct(down_weight.shape, F32),
         ),
-        in_specs=[vmem] * 5 + [hbm] * 2,
-        out_specs=(vmem, vmem, hbm, hbm),
+        in_specs=[hbm] * 7,
+        out_specs=(hbm,) * 4,
         scratch_shapes=[
+            pltpu.VMEM(merged.shape, BF16),
+            pltpu.VMEM((1, merged.shape[0]), jnp.int32),
+            pltpu.VMEM((1, merged.shape[0]), jnp.int32),
+            pltpu.VMEM((1, merged.shape[0]), F32),
+            pltpu.VMEM(mixed_grad.shape, BF16),
             pltpu.VMEM(up_weight.shape, BF16),
             pltpu.VMEM(down_weight.shape, BF16),
             pltpu.VMEM((4, 16, *block), BF16),
             pltpu.VMEM((4, 16, *block), BF16),
             pltpu.VMEM((2, 2, 4, 64, hidden), F32),
             pltpu.VMEM((2, 4, 64, hidden), F32),
-            pltpu.VMEM((2, 4, 64, hidden), F32),
-            pltpu.VMEM((2, 3, 64, hidden), F32),
+            pltpu.VMEM((2, 4, 64, hidden), BF16),
+            pltpu.VMEM((2, 3, 64, hidden), BF16),
             pltpu.VMEM((8, 64, hidden), BF16),
             pltpu.VMEM((8, 64, hidden), BF16),
             pltpu.VMEM((2, 4, 16, *block), BF16),
@@ -417,20 +494,23 @@
             pltpu.VMEM((8, 2, width), BF16),
             pltpu.VMEM((8, 2, width), BF16),
             pltpu.VMEM((8, 2, width), BF16),
+            pltpu.VMEM((2, 4, 64, hidden), F32),
+            pltpu.VMEM(mixed_grad.shape, BF16),
+            pltpu.VMEM(merged.shape, BF16),
             pltpu.VMEM(up_weight.shape, F32),
             pltpu.VMEM(down_weight.shape, F32),
-            dma((4,)),
+            dma((11,)),
             dma((2, 16)),
             dma((2, 4, 5)),
             dma((2, 2)),
             dma((2, 6, 2)),
             dma((2, 3)),
             dma((2, 2)),
-            dma((2, 6)),
+            dma((2, 8)),
             dma((2, 2)),
         ],
         compiler_params=pltpu.CompilerParams(
-            collective_id=0, has_side_effects=True, vmem_limit_bytes=48 * 1024 * 1024
+            collective_id=0, has_side_effects=True, vmem_limit_bytes=67043328
         ),
     )(
         merged,
@@ -441,6 +521,15 @@
         up_weight,
         down_weight,
     )
+    return pl.pallas_call(
+        put_out,
+        name="put_out",
+        out_shape=tuple(jax.ShapeDtypeStruct(r.shape, r.dtype) for r in results),
+        in_specs=[hbm] * 4,
+        out_specs=(hbm,) * 4,
+        scratch_shapes=[pltpu.VMEM(r.shape, r.dtype) for r in results] + [dma((2, 10))],
+        compiler_params=pltpu.CompilerParams(vmem_limit_bytes=67043328),
+    )(*results)
 
 
 def solution(mesh):

time: 90.1 us -> 82.7 us (0.918)
  local copies, waits for them, and re-layouts: 7.53 us -> 0 us
    unnamed x18 -> x0, local copies, waits for them, and re-layouts: 7.53 us -> none
    pallas_call x0 -> x1, Pallas kernels: none -> 2.46 us  [per_device(): pl.pallas_call(put_out, name='put_out', out_shape=tuple((jax.ShapeDtypeSt...]
    pallas_call x1, Pallas kernels: 80.4 us -> 78.3 us  [per_device(): pl.pallas_call(kernel, name='routed_ffn', out_shape=(jax.ShapeDtypeStruct...]
where the time goes in v2:
time: 82.7 us; the launch traced here: 81.4 us
  Pallas kernels  80.8 us (98%)
    pallas_call x1, Pallas kernels, per_device(): pl.pallas_call(kernel, name='routed_ffn', out_shape=(jax.ShapeDtypeStruct...  78.3 us
    pallas_call x1, Pallas kernels, per_device(): pl.pallas_call(put_out, name='put_out', out_shape=tuple((jax.ShapeDtypeSt...  2.46 us

profile of v2, /device:TPU:1, one launch (start us, length us, event | category | flops | bytes accessed | tf_op | source)
XLA Modules:
  0.0 81.4 jit_solution(5183281628097834601)
XLA Ops:
  0.6 78.3 %routed_ffn.1 = (bf16[16,1024]{1,0:T(8,128)(2,1)}, bf16[32,1024]{1,0:T(8,128)(2,1)}, f32[1024,256]{1,0:T(8,128)}, f32[256,1024]{1,0:T(8,128)}) custom-call(bf16[32,1024]{1,0:T(8,128)(2,1)} %merged_hbm.1, s32[1,32]{1,0:T(1,128)} %bitcast.3, s32[1,32]{1,0:T(1,128)} %bitcast.4, f32[1,32]{1,0:T(1,128)} %bitcast.5, bf16[16,1024]{1,0:T(8,128)(2,1)} %cot_hbm.1, ...), custom_call_target="tpu_custom_call" | custom-call | tf_op jit(solution)/shard_map/routed_ffn/pallas_call | solution.py:458
  78.9 2.5 %put_out.1 = (bf16[16,1024]{1,0:T(8,128)(2,1)}, bf16[32,1024]{1,0:T(8,128)(2,1)}, f32[1024,256]{1,0:T(8,128)}, f32[256,1024]{1,0:T(8,128)}) custom-call(bf16[16,1024]{1,0:T(8,128)(2,1)} %get-tuple-element.8.refs_0_, bf16[32,1024]{1,0:T(8,128)(2,1)} %get-tuple-element.9.refs_1_, f32[1024,256]{1,0:T(8,128)} %get-tuple-element.10.refs_2_, ...), custom_call_target="tpu_custom_call" | custom-call | tf_op jit(solution)/shard_map/put_out/pallas_call | solution.py:524
